TPU v7x, 32 devices: a whole 2x2x4 slice. The times are simulated.
32 devices in a mesh: dp: 32 (over z, y, x, core), tensor: 1.
Axes of the slice: x: 2, y: 2, z: 4, core: 2. Of those that a mesh axis runs over, the one named last changes fastest.
Arguments:
- latent_raw: bfloat16 [6144, 512], P('dp'), may hold values from -6 to 6
- norm_gain: float32 [512], replicated, may hold values from 0.5 to 1.5
- up_weight: bfloat16 [512, 4096], P(None, 'tensor'), may hold values from -0.25 to 0.25
- grad_kv: bfloat16 [6144, 4096], P('dp', 'tensor'), may hold values from -3 to 3
Outputs:
- latent_grad: bfloat16 [6144, 512], P('dp')
- gain_grad: float32 [512], replicated
- weight_grad: float32 [512, 4096], P('dp', 'tensor')
All inputs are finite; a program needn't handle non-finite values.
Results may differ from a plain program's by a relative error of at most 0.0029.
Values may be sent and summed in bfloat16 or wider, within the bound.
No kernel may reach another device: no remote copies, remote signals or barrier semaphores. Data moves between devices by JAX's collectives and lax.ppermute only.
A program may use at most 64 MiB of HBM per device.

v0:
```python
import jax
import jax.numpy as jnp
from jax import lax
from jax.sharding import PartitionSpec as P

epsilon = 1e-06


def normalize(latent_raw):
    latent_full = latent_raw.astype(jnp.float32)
    inverse = lax.rsqrt(jnp.mean(latent_full * latent_full, axis=-1, keepdims=True) + epsilon)
    return (latent_full * inverse, inverse)


def norm_backward(grad_norm, scaled_rows, inverse, norm_gain):
    upstream = grad_norm * norm_gain
    centred = upstream - scaled_rows * jnp.mean(upstream * scaled_rows, axis=-1, keepdims=True)
    return (inverse * centred).astype(jnp.bfloat16)


def per_device(latent_raw, norm_gain, up_weight, grad_kv):
    scaled_rows, inverse = normalize(latent_raw)
    normed = (scaled_rows * norm_gain).astype(jnp.bfloat16)
    factor = float(latent_raw.shape[0] * lax.axis_size("dp")) ** (-0.5)
    partial_norm = lax.dot_general(
        grad_kv, up_weight, (((1,), (1,)), ((), ())), preferred_element_type=jnp.float32
    )
    grad_norm = lax.psum_scatter(partial_norm, "tensor", scatter_dimension=0, tiled=True)
    row_count = grad_norm.shape[0]
    offset = lax.axis_index("tensor") * row_count
    scaled_part = lax.dynamic_slice_in_dim(scaled_rows, offset, row_count, 0)
    inverse_part = lax.dynamic_slice_in_dim(inverse, offset, row_count, 0)
    gain_local = jnp.sum(grad_norm * scaled_part, axis=0)
    latent_part = norm_backward(grad_norm, scaled_part, inverse_part, norm_gain)
    latent_grad = lax.all_gather(latent_part, "tensor", axis=0, tiled=True)
    gain_grad = lax.psum(gain_local, ("dp", "tensor")) * factor
    weight_partial = lax.dot_general(
        normed, grad_kv, (((0,), (0,)), ((), ())), preferred_element_type=jnp.float32
    )
    weight_grad = lax.psum_scatter(weight_partial, "dp", scatter_dimension=0, tiled=True) * factor
    return (latent_grad, gain_grad, weight_grad)


def solution(mesh):
    in_specs = (P("dp", None), P(), P(None, "tensor"), P("dp", "tensor"))
    out_specs = (P("dp", None), P(), P("dp", "tensor"))
    return jax.shard_map(
        per_device, mesh=mesh, in_specs=in_specs, out_specs=out_specs, check_vma=False
    )
```

profile of v0, /device:TPU:0, one launch (start us, length us, event | category | flops | bytes accessed | tf_op | source)
XLA Modules:
  0.0 175.9 jit_solution(13392894614203619147)
XLA Ops:
  7.2 0.0 copy-start
  7.2 0.0 reduce-scatter.2.cloned.1.call-start
  7.2 1.2 fusion.10
  8.4 0.3 copy-done
  8.7 5.5 %fusion.11 = f32[512,4096]{1,0:T(8,128)} fusion(bf16[192,4096]{1,0:T(8,128)(2,1)S(1)} %copy-done, bf16[192,512]{1,0:T(8,128)(2,1)} %param.4, f32[512]{0:T(512)} %param.5, f32[192]{0:T(256)S(1)} %add_rsqrt_fusion), kind=kOutput, calls=%fused_computation.13 | convolution fusion | flops 805699584 | bytes 10160896 | tf_op jit(solution)/shard_map/dot_general | solution.py:37
  14.2 0.0 copy-start.1
  14.2 0.0 copy-start.2
  14.2 0.0 reduce-scatter.2.cloned.1.call-update
  14.2 0.9 copy-done.1
  15.1 0.0 copy-done.2
  15.1 3.8 %fusion.8 = (f32[512]{0:T(512)S(1)}, f32[192]{0:T(256)S(1)}, f32[192,512]{1,0:T(8,128)S(1)}) fusion(bf16[192,512]{1,0:T(8,128)(2,1)S(1)} %copy-done.1, f32[192]{0:T(256)S(1)} %add_rsqrt_fusion, f32[512]{0:T(512)S(1)} %copy-done.2, bf16[192,4096]{1,0:T(8,128)(2,1)S(1)} %copy-done, bf16[512,4096]{1,0:T(8,128)(2,1)} %param.6), kind=kOutput, calls=%fused_computation.10 | convolution fusion | flops 805993792 | bytes 6362624 | tf_op jit(solution)/shard_map/dot_general | solution.py:25
  19.0 44.0 %psum.7 = f32[512]{0:T(512)S(1)} all-reduce(f32[512]{0:T(512)S(1)} %get-tuple-element.3), channel_id=1, replica_groups=mesh['dp'=32,'tensor'=1] {'dp','tensor'}, use_global_device_ids=true, to_apply=%region_3.0 | all-reduce | flops 512 | bytes 4096 | tf_op jit(solution)/shard_map/psum | solution.py:36
  63.0 0.6 broadcast_multiply_fusion.1
  63.6 0.9 fusion.7
  64.4 103.0 %reduce-scatter.2.cloned.1.call-done = f32[16,4096]{1,0:T(8,128)} async-done(((f32[512,4096]{1,0:T(8,128)}), f32[16,4096]{1,0:T(8,128)}) %reduce-scatter.2.cloned.1.call-update) | async-done | bytes 262160 | tf_op jit(solution)/shard_map/reduce_scatter | solution.py:40
  167.4 1.7 broadcast_multiply_fusion
  (2 shorter events, 0.0 us)
Async XLA Ops:
  7.2 1.5 copy-start
  7.2 160.2 %reduce-scatter.2.cloned.1.call-start = ((), (), s32[]{:S(2)}) async-start(), calls=%async_computation.1 | async-start | bytes 8650752 | tf_op jit(solution)/shard_map/reduce_scatter | solution.py:40
  14.2 0.9 copy-start.1
  14.2 0.9 copy-start.2
Sparse Core Ops, SparseCore 0:
  14.3 153.0 reduce-scatter.1
where the time goes:
time: 176 us
  waiting for transfers between devices  103 us (59%)
  blocking collectives  44 us (25%)
  between operations  14.1 us (8%)
  matrix products  9.36 us (5%)
  other arithmetic  4.27 us (2%)
    reduce_scatter x1, waiting for transfers between devices, per_device(): lax.psum_scatter(weight_partial, 'dp', scatter_dimension=0, tiled=True)  103 us
    psum x1, blocking collectives, per_device(): gain_grad = lax.psum(gain_local, ('dp', 'tensor')) * factor  44 us
    dot_general x1, matrix products, per_device(): lax.dot_general(normed, grad_kv, (((0,), (0,)), ((), ())), preferred_elem...  5.52 us
    dot_general x1, matrix products, per_device(): lax.dot_general(grad_kv, up_weight, (((1,), (1,)), ((), ())), preferred_e...  3.83 us
  transfers between devices with their start and end apart: 1, of which 1 were waited for; matrix products, arithmetic and copies ran while one was open for 3% of the time, Pallas kernels for 0%

commit v1 on v0

--- a/solution.py
+++ b/solution.py
@@ -19,6 +19,11 @@
 
 
 def per_device(latent_raw, norm_gain, up_weight, grad_kv):
+
+    def _track_notes(sheet, axis_name):
+        f_next = jnp.sum(lax.all_gather(sheet, axis_name), axis=0)
+        return f_next
+
     scaled_rows, inverse = normalize(latent_raw)
     normed = (scaled_rows * norm_gain).astype(jnp.bfloat16)
     factor = float(latent_raw.shape[0] * lax.axis_size("dp")) ** (-0.5)
@@ -33,7 +38,7 @@
     gain_local = jnp.sum(grad_norm * scaled_part, axis=0)
     latent_part = norm_backward(grad_norm, scaled_part, inverse_part, norm_gain)
     latent_grad = lax.all_gather(latent_part, "tensor", axis=0, tiled=True)
-    gain_grad = lax.psum(gain_local, ("dp", "tensor")) * factor
+    gain_grad = _track_notes(gain_local, axis_name=("dp", "tensor")) * factor
     weight_partial = lax.dot_general(
         normed, grad_kv, (((0,), (0,)), ((), ())), preferred_element_type=jnp.float32
     )

time: 176 us -> 176 us (level)
    psum x1 -> x0, blocking collectives: 44 us -> none  [per_device(): gain_grad = lax.psum(gain_local, ('dp', 'tensor')) * factor]
    all_gather x0 -> x1, blocking collectives: none -> 43.6 us  [_track_notes(): f_next = jnp.sum(lax.all_gather(sheet, axis_name), axis=0)]
where the time goes in v1:
time: 176 us
  waiting for transfers between devices  103 us (59%)
  blocking collectives  43.6 us (25%)
  between operations  14.1 us (8%)
  matrix products  9.36 us (5%)
  other arithmetic  4.34 us (2%)
    reduce_scatter x1, waiting for transfers between devices, per_device(): lax.psum_scatter(weight_partial, 'dp', scatter_dimension=0, tiled=True)  103 us
    all_gather x1, blocking collectives, _track_notes(): f_next = jnp.sum(lax.all_gather(sheet, axis_name), axis=0)  43.6 us
    dot_general x1, matrix products, per_device(): lax.dot_general(normed, grad_kv, (((0,), (0,)), ((), ())), preferred_elem...  5.52 us
    dot_general x1, matrix products, per_device(): lax.dot_general(grad_kv, up_weight, (((1,), (1,)), ((), ())), preferred_e...  3.83 us
  transfers between devices with their start and end apart: 1, of which 1 were waited for; matrix products, arithmetic and copies ran while one was open for 3% of the time, Pallas kernels for 0%

profile of v1, /device:TPU:0, one launch (start us, length us, event | category | flops | bytes accessed | tf_op | source)
XLA Modules:
  0.0 175.9 jit_solution(3146325256524454540)
XLA Ops:
  7.2 0.0 copy-start
  7.2 0.0 reduce-scatter.2.cloned.1.call-start
  7.2 1.2 fusion.10
  8.4 0.3 copy-done
  8.7 5.5 %fusion.11 = f32[512,4096]{1,0:T(8,128)} fusion(bf16[192,4096]{1,0:T(8,128)(2,1)S(1)} %copy-done, bf16[192,512]{1,0:T(8,128)(2,1)} %param.4, f32[512]{0:T(512)} %param.5, f32[192]{0:T(256)S(1)} %add_rsqrt_fusion), kind=kOutput, calls=%fused_computation.13 | convolution fusion | flops 805699584 | bytes 10160896 | tf_op jit(solution)/shard_map/dot_general | solution.py:42
  14.2 0.0 copy-start.1
  14.2 0.0 copy-start.2
  14.2 0.0 reduce-scatter.2.cloned.1.call-update
  14.2 0.9 copy-done.1
  15.1 0.0 copy-done.2
  15.1 3.8 %fusion.8 = (f32[512]{0:T(512)S(1)}, f32[192]{0:T(256)S(1)}, f32[192,512]{1,0:T(8,128)S(1)}) fusion(bf16[192,512]{1,0:T(8,128)(2,1)S(1)} %copy-done.1, f32[192]{0:T(256)S(1)} %add_rsqrt_fusion, f32[512]{0:T(512)S(1)} %copy-done.2, bf16[192,4096]{1,0:T(8,128)(2,1)S(1)} %copy-done, bf16[512,4096]{1,0:T(8,128)(2,1)} %param.6), kind=kOutput, calls=%fused_computation.10 | convolution fusion | flops 805993792 | bytes 6362624 | tf_op jit(solution)/shard_map/dot_general | solution.py:30
  19.0 43.6 %all-gather.1 = f32[32,1,512]{2,1,0:T(1,128)S(1)} all-gather(f32[1,1,512]{2,1,0:T(1,128)S(1)} %bitcast.4), channel_id=2, replica_groups=mesh['dp'=32,'tensor'=1] {'dp','tensor'}, dimensions={0}, use_global_device_ids=true | all-gather | bytes 67584 | tf_op jit(solution)/shard_map/all_gather | solution.py:24
  62.6 0.1 reduce_sum.39
  62.6 0.6 broadcast_multiply_fusion.1
  63.2 0.9 fusion.7
  64.1 103.3 %reduce-scatter.2.cloned.1.call-done = f32[16,4096]{1,0:T(8,128)} async-done(((f32[512,4096]{1,0:T(8,128)}), f32[16,4096]{1,0:T(8,128)}) %reduce-scatter.2.cloned.1.call-update) | async-done | bytes 262160 | tf_op jit(solution)/shard_map/reduce_scatter | solution.py:45
  167.3 1.7 broadcast_multiply_fusion
  (2 shorter events, 0.0 us)
Async XLA Ops:
  7.2 1.5 copy-start
  7.2 160.2 %reduce-scatter.2.cloned.1.call-start = ((), (), s32[]{:S(2)}) async-start(), calls=%async_computation.1 | async-start | bytes 8650752 | tf_op jit(solution)/shard_map/reduce_scatter | solution.py:45
  14.2 0.9 copy-start.1
  14.2 0.9 copy-start.2
Sparse Core Ops, SparseCore 0:
  14.3 152.9 reduce-scatter.1
